TPU v7x, 32 devices: a whole 2x2x4 slice. The times are simulated.
32 devices in a mesh: traj: 16 (over z, y, core), tm: 2 (over x).
Axes of the slice: x: 2, y: 2, z: 4, core: 2. Of those that a mesh axis runs over, the one named last changes fastest.
Arguments:
- states: float32 [2, 32, 4096], P('tm', None, 'traj'), may hold values from -6 to 6
- vectors: bfloat16 [64, 4096], P(None, 'traj'), may hold values from -6 to 6
- kernel_scale: float32 [2], P('tm'), may hold values from 6 to 16
- neighbour_blocks: int32 [32, 24], P('traj'), may hold values from 0 to 31, as said below
- neighbour_count: int32 [32], P('traj'), may hold values from 6 to 24, as said below
Outputs:
- result: float32 [64, 4096], P(None, 'traj')
Inputs may be any that keep to these rules, and one draw needn't show every extreme that they name: `neighbour_blocks`: row b names 24 different blocks, the first of them b itself. Only the first neighbour_count[b] entries of row b of neighbour_blocks are neighbours of block b; some block uses all 24.
All inputs are finite; a program needn't handle non-finite values.
Results may differ from a plain program's by a relative error of at most 0.0013.
Values may be sent and summed in bfloat16 or wider, within the bound.
No kernel may reach another device: no remote copies, remote signals or barrier semaphores. Data moves between devices by JAX's collectives and lax.ppermute only.
A program may use at most 64 MiB of HBM per device.

v0:
```python
import math
import jax
import jax.numpy as jnp
from jax import lax
from jax.sharding import PartitionSpec as P

BLK = 128


def linked_blocks(neighbour_blocks, neighbour_count, blocks_total):
    slots = neighbour_blocks.shape[1]
    named = neighbour_blocks[:, :, None] == jnp.arange(blocks_total, dtype=jnp.int32)[None, None, :]
    within = jnp.arange(slots, dtype=jnp.int32)[None, :, None] < neighbour_count[:, None, None]
    return jnp.any(named & within, axis=1).astype(jnp.float32)


def per_device(states, vectors, kernel_scale, neighbour_blocks, neighbour_count):
    coords_all = lax.all_gather(states, "traj", axis=2, tiled=True)[0]
    vectors_all = lax.all_gather(vectors, "traj", axis=1, tiled=True)
    own = states[0]
    spread = kernel_scale[0]
    own_rows = own.shape[1]
    columns = coords_all.shape[1]
    vector_count = vectors.shape[0]
    blocks_total = columns // BLK
    block_rows = own_rows // BLK
    own_squares = jnp.sum(own * own, axis=0)
    all_squares = jnp.sum(coords_all * coords_all, axis=0)
    tile_width = math.gcd(columns, 512)
    tile_count = columns // tile_width
    linked = linked_blocks(neighbour_blocks, neighbour_count, blocks_total)

    def dense_kernel(tile_index):
        offset = tile_index * tile_width
        slab = lax.dynamic_slice_in_dim(coords_all, offset, tile_width, 1)
        cross = lax.dot_general(
            own, slab, (((0,), (0,)), ((), ())), precision=lax.Precision.HIGHEST
        )
        slab_squares = lax.dynamic_slice_in_dim(all_squares, offset, tile_width, 0)
        distance = own_squares[:, None] + slab_squares[None, :] - 2.0 * cross
        mask = lax.dynamic_slice_in_dim(linked, offset // BLK, tile_width // BLK, 1)
        shaped = jnp.exp(-distance / spread).reshape(block_rows, BLK, tile_width // BLK, BLK)
        return (mask[:, None, :, None] * shaped).reshape(own_rows, tile_width)

    def first_dense(tile_index, carry):
        row_sum, pushed = carry
        kernel = dense_kernel(tile_index)
        weights = kernel.astype(jnp.bfloat16)
        slab_vectors = lax.dynamic_slice_in_dim(vectors_all, tile_index * tile_width, tile_width, 1)
        pushed = pushed + lax.dot_general(
            slab_vectors, weights, (((1,), (1,)), ((), ())), preferred_element_type=jnp.float32
        )
        return (row_sum + jnp.sum(kernel, axis=1), pushed)

    row_sum, pushed = lax.fori_loop(
        0,
        tile_count,
        first_dense,
        (jnp.zeros((own_rows,), jnp.float32), jnp.zeros((vector_count, own_rows), jnp.float32)),
    )
    scaled = (pushed / (row_sum * row_sum)[None, :]).astype(jnp.bfloat16)
    lists_whole, counts_whole = (
        lax.all_gather(neighbour_blocks, "traj", axis=0, tiled=True),
        lax.all_gather(neighbour_count, "traj", axis=0, tiled=True),
    )
    linked_whole = linked_blocks(lists_whole, counts_whole, blocks_total)
    own_start = lax.axis_index("traj") * block_rows
    column_mask = lax.dynamic_slice_in_dim(linked_whole, own_start, block_rows, 1)
    scaled_whole = lax.all_gather(scaled, "traj", axis=1, tiled=True)

    def pull_tile(tile_index, total):
        offset = tile_index * tile_width
        slab = lax.dynamic_slice_in_dim(coords_all, offset, tile_width, 1)
        cross = lax.dot_general(
            slab, own, (((0,), (0,)), ((), ())), precision=lax.Precision.HIGHEST
        )
        slab_squares = lax.dynamic_slice_in_dim(all_squares, offset, tile_width, 0)
        distance = slab_squares[:, None] + own_squares[None, :] - 2.0 * cross
        mask = lax.dynamic_slice_in_dim(column_mask, offset // BLK, tile_width // BLK, 0)
        shaped = jnp.exp(-distance / spread).reshape(tile_width // BLK, BLK, block_rows, BLK)
        weights = (
            (mask[:, None, :, None] * shaped).reshape(tile_width, own_rows).astype(jnp.bfloat16)
        )
        slab_scaled = lax.dynamic_slice_in_dim(scaled_whole, offset, tile_width, 1)
        return total + jnp.dot(slab_scaled, weights, preferred_element_type=jnp.float32)

    own_pulled = lax.fori_loop(
        0, tile_count, pull_tile, jnp.zeros((vector_count, own_rows), jnp.float32)
    )
    result = lax.psum(own_pulled, "tm")
    return result


def solution(mesh):
    in_specs = (P("tm", None, "traj"), P(None, "traj"), P("tm"), P("traj", None), P("traj"))
    out_specs = P(None, "traj")
    return jax.shard_map(
        per_device, mesh=mesh, in_specs=in_specs, out_specs=out_specs, check_vma=False
    )
```

profile of v0, /device:TPU:0, one launch (start us, length us, event | category | flops | bytes accessed | tf_op | source)
XLA Modules:
  0.0 164.4 jit_solution(14845167993915511679)
XLA Ops:
  6.5 24.9 %all_gather.15 = f32[1,32,4096]{2,1,0:T(8,128)S(1)} all-gather(f32[1,32,256]{2,1,0:T(8,128)} %param.9), channel_id=1, replica_groups=mesh['traj'=16,'tm'=2] {'traj'}, dimensions={2}, use_global_device_ids=true | all-gather | bytes 557056 | tf_op jit(solution)/shard_map/all_gather | solution.py:18
  31.6 0.7 copy-done.2
  32.3 19.0 %all_gather.16 = bf16[64,4096]{1,0:T(8,128)(2,1)S(1)} all-gather(bf16[64,256]{1,0:T(8,128)(2,1)S(1)} %copy-done.2), channel_id=1, replica_groups=mesh['traj'=16,'tm'=2] {'traj'}, dimensions={1}, use_global_device_ids=true | all-gather | bytes 557056 | tf_op jit(solution)/shard_map/all_gather | solution.py:19
  51.4 0.6 copy-done.3
  52.1 17.0 %while.34 = (s32[]{:T(128)}, f32[256]{0:T(256)S(1)}, f32[64,256]{1,0:T(8,128)S(1)}, f32[2,32]{1,0:T(2,128)S(1)}, f32[256]{0:T(256)S(1)}, /*index=5*/f32[4096]{0:...) while((s32[]{:T(128)}, f32[256]{0:T(256)S(1)}, ...), condition=%wide.region_6.7_spmd.clone, body=%wide.region_4.0_spmd.clone.sunk | while | flops 68190488 | bytes 1879617 | solution.py:55
  52.6 1.4 fusion.42
  54.7 1.4 fusion.42
  56.8 1.4 fusion.42
  59.0 1.4 fusion.42
  61.1 1.4 fusion.42
  63.2 1.4 fusion.42
  65.4 1.4 fusion.42
  67.5 1.4 fusion.42
  69.1 20.3 %all_gather.17 = bf16[64,4096]{1,0:T(8,128)(2,1)S(1)} all-gather(bf16[64,256]{1,0:T(8,128)(2,1)S(1)} %divide_convert_fusion), channel_id=1, replica_groups=mesh['traj'=16,'tm'=2] {'traj'}, dimensions={1}, use_global_device_ids=true | all-gather | bytes 557056 | tf_op jit(solution)/shard_map/all_gather | solution.py:69
  89.5 0.7 copy-done.5
  90.1 0.7 dynamic-slice
  91.5 0.2 dynamic-update-slice
  91.7 8.0 %all-reduce = s32[32]{0:T(128)S(1)} all-reduce(s32[32]{0:T(128)S(1)} %dynamic-update-slice), channel_id=1, replica_groups=mesh['traj'=16,'tm'=2] {'traj'}, use_global_device_ids=true, to_apply=%add | all-reduce | flops 32 | bytes 256
  99.8 21.6 %all-gather = s32[16,2,24]{2,1,0:T(2,128)S(1)} all-gather(s32[1,2,24]{2,1,0:T(2,128)S(1)} %bitcast.53), channel_id=1, replica_groups=mesh['traj'=16,'tm'=2] {'traj'}, dimensions={0}, use_global_device_ids=true | all-gather | bytes 3264 | tf_op jit(solution)/shard_map/all_gather | solution.py:63
  121.3 0.3 fusion.22
  121.7 15.4 %while.35 = (s32[]{:T(128)}, f32[64,256]{1,0:T(8,128)S(1)}, bf16[64,4096]{1,0:T(8,128)(2,1)S(1)}, f32[32,2]{1,0:T(8,128)S(1)}, f32[4096]{0:T(1024)S(1)}, /*index...) while((s32[]{:T(128)}, f32[64,256]{1,0:T(8,128)S(1)}, ...), condition=%wide.region_8.9_spmd.clone, body=%wide.region_7.8_spmd.clone.sunk | while | flops 68059160 | bytes 1875448 | solution.py:87
  122.0 1.4 fusion.47
  124.0 1.4 fusion.47
  125.9 1.4 fusion.47
  127.8 1.4 fusion.47
  129.8 1.4 fusion.47
  131.7 1.4 fusion.47
  133.6 1.4 fusion.47
  135.5 1.4 fusion.47
  137.1 0.6 copy-done
  137.8 18.3 %all-reduce.3.cloned.1.call-done = f32[64,256]{1,0:T(8,128)} async-done(((f32[64,256]{1,0:T(8,128)}), f32[64,256]{1,0:T(8,128)}) %all-reduce.3.cloned.1.call-update) | async-done | bytes 65552 | tf_op jit(solution)/shard_map/psum | solution.py:90
  156.1 1.5 copy.35
  (103 shorter events, 9.5 us)
Async XLA Ops:
  6.5 24.9 %copy-start.1 = (f32[1,32,256]{2,1,0:T(8,128)S(1)}, f32[1,32,256]{2,1,0:T(8,128)}, u32[]{:S(2)}) copy-start(f32[1,32,256]{2,1,0:T(8,128)} %param.9) | copy-start | bytes 98308
  6.5 149.6 %all-reduce.3.cloned.1.call-start = ((), (), s32[]{:S(2)}) async-start(), calls=%async_computation | async-start | bytes 131072 | tf_op jit(solution)/shard_map/psum | solution.py:90
  31.5 0.8 copy-start.2
  32.3 19.0 %copy-start.4 = (s32[2]{0:T(128)S(1)}, s32[2]{0:T(128)}, u32[]{:S(2)}) copy-start(s32[2]{0:T(128)} %param.13) | copy-start | bytes 28
  51.3 0.7 copy-start.3
  89.5 0.7 copy-start.5
  137.1 0.6 copy-start
Sparse Core Ops, SparseCore 0:
  137.9 18.1 all-reduce.2
where the time goes:
time: 165 us; the launch traced here: 164 us
  blocking collectives  93.8 us (57%)
  matrix products  25.1 us (15%)
  waiting for transfers between devices  18.4 us (11%)
  between operations  14.2 us (9%)
  local copies, waits for them, and re-layouts  10.9 us (7%)
    all_gather x1, blocking collectives, per_device(): coords_all = lax.all_gather(states, 'traj', axis=2, tiled=True)[0]  24.9 us
    all_gather x1, blocking collectives, per_device(): lax.all_gather(neighbour_blocks, 'traj', axis=0, tiled=True)  21.6 us
    all_gather x1, blocking collectives, per_device(): scaled_whole = lax.all_gather(scaled, 'traj', axis=1, tiled=True)  20.3 us
    all_gather x1, blocking collectives, per_device(): vectors_all = lax.all_gather(vectors, 'traj', axis=1, tiled=True)  19 us
    psum x1, waiting for transfers between devices, per_device(): result = lax.psum(own_pulled, 'tm')  18.3 us
    dot_general x8, matrix products, dense_kernel(): lax.dot_general(own, slab, (((0,), (0,)), ((), ())), precision=lax.Precis...  11.2 us
    dot_general x8, matrix products, pull_tile(): lax.dot_general(slab, own, (((0,), (0,)), ((), ())), precision=lax.Precis...  10.9 us
    unnamed x1, blocking collectives  7.97 us
  transfers between devices with their start and end apart: 1, of which 1 were waited for; matrix products, arithmetic and copies ran while one was open for 0% of the time, Pallas kernels for 0%

commit v1 on v0

--- a/solution.py
+++ b/solution.py
@@ -87,7 +87,7 @@
     own_pulled = lax.fori_loop(
         0, tile_count, pull_tile, jnp.zeros((vector_count, own_rows), jnp.float32)
     )
-    result = lax.psum(own_pulled, "tm")
+    result = lax.all_gather(own_pulled, axis_name="tm").sum(axis=0)
     return result
 
 

time: 165 us -> 137 us (0.83)
  waiting for transfers between devices: 18.4 us -> 0 us
  between operations: 14.2 us -> 0.73 us
  blocking collectives: 93.8 us -> 98.5 us
    psum x1 -> x0, waiting for transfers between devices: 18.3 us -> none  [per_device(): result = lax.psum(own_pulled, 'tm')]
    all_gather x0 -> x1, blocking collectives: none -> 5 us  [per_device(): result = lax.all_gather(own_pulled, axis_name='tm').sum(axis=0)]
    unnamed x16 -> x13, local copies, waits for them, and re-layouts: 4.95 us -> 3.47 us
  transfers between devices with their start and end apart: 1 -> 0, of which waited for: 1 -> 0; matrix products, arithmetic and copies ran while one was open for 0% -> 0% of each run, Pallas kernels for 0% -> 0%
where the time goes in v1:
time: 137 us
  blocking collectives  98.5 us (72%)
  matrix products  25.1 us (18%)
  local copies, waits for them, and re-layouts  9.42 us (7%)
  other arithmetic  1.46 us (1%)
    all_gather x1, blocking collectives, per_device(): coords_all = lax.all_gather(states, 'traj', axis=2, tiled=True)[0]  24.8 us
    all_gather x1, blocking collectives, per_device(): lax.all_gather(neighbour_blocks, 'traj', axis=0, tiled=True)  21.6 us
    all_gather x1, blocking collectives, per_device(): scaled_whole = lax.all_gather(scaled, 'traj', axis=1, tiled=True)  20.3 us
    all_gather x1, blocking collectives, per_device(): vectors_all = lax.all_gather(vectors, 'traj', axis=1, tiled=True)  18.9 us
    dot_general x8, matrix products, dense_kernel(): lax.dot_general(own, slab, (((0,), (0,)), ((), ())), precision=lax.Precis...  11.2 us
    dot_general x8, matrix products, pull_tile(): lax.dot_general(slab, own, (((0,), (0,)), ((), ())), precision=lax.Precis...  10.9 us
    unnamed x1, blocking collectives  7.97 us
    all_gather x1, blocking collectives, per_device(): result = lax.all_gather(own_pulled, axis_name='tm').sum(axis=0)  5 us

profile of v1, /device:TPU:0, one launch (start us, length us, event | category | flops | bytes accessed | tf_op | source)
XLA Modules:
  0.0 136.5 jit_solution(8495151865991509928)
XLA Ops:
  0.0 24.8 %all_gather.21 = f32[1,32,4096]{2,1,0:T(8,128)S(1)} all-gather(f32[1,32,256]{2,1,0:T(8,128)} %param.9), channel_id=1, replica_groups=mesh['traj'=16,'tm'=2] {'traj'}, dimensions={2}, use_global_device_ids=true | all-gather | bytes 557056 | tf_op jit(solution)/shard_map/all_gather | solution.py:18
  24.9 0.7 copy-done
  25.6 18.9 %all_gather.22 = bf16[64,4096]{1,0:T(8,128)(2,1)S(1)} all-gather(bf16[64,256]{1,0:T(8,128)(2,1)S(1)} %copy-done.1), channel_id=1, replica_groups=mesh['traj'=16,'tm'=2] {'traj'}, dimensions={1}, use_global_device_ids=true | all-gather | bytes 557056 | tf_op jit(solution)/shard_map/all_gather | solution.py:19
  44.5 0.7 copy-done.3
  45.2 0.6 copy-done.2
  45.9 17.0 %while.34 = (s32[]{:T(128)}, f32[256]{0:T(256)S(1)}, f32[64,256]{1,0:T(8,128)S(1)}, f32[2,32]{1,0:T(2,128)S(1)}, f32[256]{0:T(256)S(1)}, /*index=5*/f32[4096]{0:...) while((s32[]{:T(128)}, f32[256]{0:T(256)S(1)}, ...), condition=%wide.region_6.7_spmd.clone, body=%wide.region_4.0_spmd.clone.sunk | while | flops 68190488 | bytes 1879617 | solution.py:55
  46.5 1.4 %fusion.42 = (f32[256]{0:T(256)S(1)}, bf16[256,512]{0,1:T(8,128)(2,1)S(1)}) fusion(f32[]{:T(128)} %get-tuple-element.752, f32[32,256]{1,0:T(8,128)S(1)} %get-tuple-element.751, f32[32,4096]{1,0:T(8,128)S(1)} %get-tuple-element.750, s32[]{:T(128)S(6)} %select_n.82, f32[512]{0:T(512)S(1)} %dynamic_slice.117, f32[256]{0:T(256)S(1)} %get-tuple-element.748, ...), kind=kOutput, calls=%fused_computation.40.clone.1 | convolution fusion | flops 51379968 | bytes 888840 | tf_op jit(solution)/shard_map/while/body/eval_jaxpr/dot_general | solution.py:36
  48.6 1.4 %fusion.42 = (f32[256]{0:T(256)S(1)}, bf16[256,512]{0,1:T(8,128)(2,1)S(1)}) fusion(f32[]{:T(128)} %get-tuple-element.752, f32[32,256]{1,0:T(8,128)S(1)} %get-tuple-element.751, f32[32,4096]{1,0:T(8,128)S(1)} %get-tuple-element.750, s32[]{:T(128)S(6)} %select_n.82, f32[512]{0:T(512)S(1)} %dynamic_slice.117, f32[256]{0:T(256)S(1)} %get-tuple-element.748, ...), kind=kOutput, calls=%fused_computation.40.clone.1 | convolution fusion | flops 51379968 | bytes 888840 | tf_op jit(solution)/shard_map/while/body/eval_jaxpr/dot_general | solution.py:36
  50.7 1.4 %fusion.42 = (f32[256]{0:T(256)S(1)}, bf16[256,512]{0,1:T(8,128)(2,1)S(1)}) fusion(f32[]{:T(128)} %get-tuple-element.752, f32[32,256]{1,0:T(8,128)S(1)} %get-tuple-element.751, f32[32,4096]{1,0:T(8,128)S(1)} %get-tuple-element.750, s32[]{:T(128)S(6)} %select_n.82, f32[512]{0:T(512)S(1)} %dynamic_slice.117, f32[256]{0:T(256)S(1)} %get-tuple-element.748, ...), kind=kOutput, calls=%fused_computation.40.clone.1 | convolution fusion | flops 51379968 | bytes 888840 | tf_op jit(solution)/shard_map/while/body/eval_jaxpr/dot_general | solution.py:36
  52.8 1.4 %fusion.42 = (f32[256]{0:T(256)S(1)}, bf16[256,512]{0,1:T(8,128)(2,1)S(1)}) fusion(f32[]{:T(128)} %get-tuple-element.752, f32[32,256]{1,0:T(8,128)S(1)} %get-tuple-element.751, f32[32,4096]{1,0:T(8,128)S(1)} %get-tuple-element.750, s32[]{:T(128)S(6)} %select_n.82, f32[512]{0:T(512)S(1)} %dynamic_slice.117, f32[256]{0:T(256)S(1)} %get-tuple-element.748, ...), kind=kOutput, calls=%fused_computation.40.clone.1 | convolution fusion | flops 51379968 | bytes 888840 | tf_op jit(solution)/shard_map/while/body/eval_jaxpr/dot_general | solution.py:36
  55.0 1.4 %fusion.42 = (f32[256]{0:T(256)S(1)}, bf16[256,512]{0,1:T(8,128)(2,1)S(1)}) fusion(f32[]{:T(128)} %get-tuple-element.752, f32[32,256]{1,0:T(8,128)S(1)} %get-tuple-element.751, f32[32,4096]{1,0:T(8,128)S(1)} %get-tuple-element.750, s32[]{:T(128)S(6)} %select_n.82, f32[512]{0:T(512)S(1)} %dynamic_slice.117, f32[256]{0:T(256)S(1)} %get-tuple-element.748, ...), kind=kOutput, calls=%fused_computation.40.clone.1 | convolution fusion | flops 51379968 | bytes 888840 | tf_op jit(solution)/shard_map/while/body/eval_jaxpr/dot_general | solution.py:36
  57.1 1.4 %fusion.42 = (f32[256]{0:T(256)S(1)}, bf16[256,512]{0,1:T(8,128)(2,1)S(1)}) fusion(f32[]{:T(128)} %get-tuple-element.752, f32[32,256]{1,0:T(8,128)S(1)} %get-tuple-element.751, f32[32,4096]{1,0:T(8,128)S(1)} %get-tuple-element.750, s32[]{:T(128)S(6)} %select_n.82, f32[512]{0:T(512)S(1)} %dynamic_slice.117, f32[256]{0:T(256)S(1)} %get-tuple-element.748, ...), kind=kOutput, calls=%fused_computation.40.clone.1 | convolution fusion | flops 51379968 | bytes 888840 | tf_op jit(solution)/shard_map/while/body/eval_jaxpr/dot_general | solution.py:36
  59.2 1.4 %fusion.42 = (f32[256]{0:T(256)S(1)}, bf16[256,512]{0,1:T(8,128)(2,1)S(1)}) fusion(f32[]{:T(128)} %get-tuple-element.752, f32[32,256]{1,0:T(8,128)S(1)} %get-tuple-element.751, f32[32,4096]{1,0:T(8,128)S(1)} %get-tuple-element.750, s32[]{:T(128)S(6)} %select_n.82, f32[512]{0:T(512)S(1)} %dynamic_slice.117, f32[256]{0:T(256)S(1)} %get-tuple-element.748, ...), kind=kOutput, calls=%fused_computation.40.clone.1 | convolution fusion | flops 51379968 | bytes 888840 | tf_op jit(solution)/shard_map/while/body/eval_jaxpr/dot_general | solution.py:36
  61.4 1.4 %fusion.42 = (f32[256]{0:T(256)S(1)}, bf16[256,512]{0,1:T(8,128)(2,1)S(1)}) fusion(f32[]{:T(128)} %get-tuple-element.752, f32[32,256]{1,0:T(8,128)S(1)} %get-tuple-element.751, f32[32,4096]{1,0:T(8,128)S(1)} %get-tuple-element.750, s32[]{:T(128)S(6)} %select_n.82, f32[512]{0:T(512)S(1)} %dynamic_slice.117, f32[256]{0:T(256)S(1)} %get-tuple-element.748, ...), kind=kOutput, calls=%fused_computation.40.clone.1 | convolution fusion | flops 51379968 | bytes 888840 | tf_op jit(solution)/shard_map/while/body/eval_jaxpr/dot_general | solution.py:36
  63.0 20.3 %all_gather.23 = bf16[64,4096]{1,0:T(8,128)(2,1)S(1)} all-gather(bf16[64,256]{1,0:T(8,128)(2,1)S(1)} %divide_convert_fusion), channel_id=1, replica_groups=mesh['traj'=16,'tm'=2] {'traj'}, dimensions={1}, use_global_device_ids=true | all-gather | bytes 557056 | tf_op jit(solution)/shard_map/all_gather | solution.py:69
  83.3 0.7 copy-done.4
  84.0 0.6 dynamic-slice
  85.2 0.2 dynamic-update-slice
  85.5 8.0 %all-reduce = s32[32]{0:T(128)S(1)} all-reduce(s32[32]{0:T(128)S(1)} %dynamic-update-slice), channel_id=1, replica_groups=mesh['traj'=16,'tm'=2] {'traj'}, use_global_device_ids=true, to_apply=%add | all-reduce | flops 32 | bytes 256
  93.5 21.6 %all-gather.1 = s32[16,2,24]{2,1,0:T(2,128)S(1)} all-gather(s32[1,2,24]{2,1,0:T(2,128)S(1)} %bitcast.55), channel_id=1, replica_groups=mesh['traj'=16,'tm'=2] {'traj'}, dimensions={0}, use_global_device_ids=true | all-gather | bytes 3264 | tf_op jit(solution)/shard_map/all_gather | solution.py:63
  115.1 0.3 fusion.22
  115.5 15.4 %while.35 = (s32[]{:T(128)}, f32[64,256]{1,0:T(8,128)S(1)}, bf16[64,4096]{1,0:T(8,128)(2,1)S(1)}, f32[32,2]{1,0:T(8,128)S(1)}, f32[4096]{0:T(1024)S(1)}, /*index...) while((s32[]{:T(128)}, f32[64,256]{1,0:T(8,128)S(1)}, ...), condition=%wide.region_8.9_spmd.clone, body=%wide.region_7.8_spmd.clone.sunk | while | flops 68059160 | bytes 1875448 | solution.py:87
  115.8 1.4 fusion.47
  117.7 1.4 %fusion.47 = bf16[512,256]{1,0:T(8,128)(2,1)S(1)} fusion(f32[32,256]{1,0:T(8,128)S(1)} %get-tuple-element.803, f32[64,8,2,128]{3,2,1,0:T(2,128)S(1)} %bitcast.50, f32[]{:T(128)} %get-tuple-element.804, f32[256]{0:T(256)S(1)} %get-tuple-element.801, f32[512]{0:T(512)S(1)} %dynamic_slice.121, f32[32,4096]{1,0:T(8,128)S(1)} %get-tuple-element.802, ...), kind=kOutput, calls=%fused_computation.21.clone.1 | convolution fusion | flops 51249152 | bytes 887816 | tf_op jit(solution)/shard_map/while/body/eval_jaxpr/dot_general | solution.py:74
  119.6 1.4 %fusion.47 = bf16[512,256]{1,0:T(8,128)(2,1)S(1)} fusion(f32[32,256]{1,0:T(8,128)S(1)} %get-tuple-element.803, f32[64,8,2,128]{3,2,1,0:T(2,128)S(1)} %bitcast.50, f32[]{:T(128)} %get-tuple-element.804, f32[256]{0:T(256)S(1)} %get-tuple-element.801, f32[512]{0:T(512)S(1)} %dynamic_slice.121, f32[32,4096]{1,0:T(8,128)S(1)} %get-tuple-element.802, ...), kind=kOutput, calls=%fused_computation.21.clone.1 | convolution fusion | flops 51249152 | bytes 887816 | tf_op jit(solution)/shard_map/while/body/eval_jaxpr/dot_general | solution.py:74
  121.6 1.4 fusion.47
  123.5 1.4 fusion.47
  125.4 1.4 %fusion.47 = bf16[512,256]{1,0:T(8,128)(2,1)S(1)} fusion(f32[32,256]{1,0:T(8,128)S(1)} %get-tuple-element.803, f32[64,8,2,128]{3,2,1,0:T(2,128)S(1)} %bitcast.50, f32[]{:T(128)} %get-tuple-element.804, f32[256]{0:T(256)S(1)} %get-tuple-element.801, f32[512]{0:T(512)S(1)} %dynamic_slice.121, f32[32,4096]{1,0:T(8,128)S(1)} %get-tuple-element.802, ...), kind=kOutput, calls=%fused_computation.21.clone.1 | convolution fusion | flops 51249152 | bytes 887816 | tf_op jit(solution)/shard_map/while/body/eval_jaxpr/dot_general | solution.py:74
  127.4 1.4 %fusion.47 = bf16[512,256]{1,0:T(8,128)(2,1)S(1)} fusion(f32[32,256]{1,0:T(8,128)S(1)} %get-tuple-element.803, f32[64,8,2,128]{3,2,1,0:T(2,128)S(1)} %bitcast.50, f32[]{:T(128)} %get-tuple-element.804, f32[256]{0:T(256)S(1)} %get-tuple-element.801, f32[512]{0:T(512)S(1)} %dynamic_slice.121, f32[32,4096]{1,0:T(8,128)S(1)} %get-tuple-element.802, ...), kind=kOutput, calls=%fused_computation.21.clone.1 | convolution fusion | flops 51249152 | bytes 887816 | tf_op jit(solution)/shard_map/while/body/eval_jaxpr/dot_general | solution.py:74
  129.3 1.4 fusion.47
  130.9 5.0 %all-gather = f32[128,256]{1,0:T(8,128)S(1)} all-gather(f32[64,256]{1,0:T(8,128)S(1)} %get-tuple-element.472), channel_id=2, replica_groups=mesh['traj'=16,'tm'=2] {'tm'}, dimensions={0}, use_global_device_ids=true | all-gather | bytes 196608 | tf_op jit(solution)/shard_map/all_gather | solution.py:90
  135.9 0.6 reduce_sum.45
  (99 shorter events, 9.6 us)
Async XLA Ops:
  24.8 0.8 copy-start
  24.9 0.8 copy-start.1
  44.5 0.7 copy-start.3
  45.2 0.7 copy-start.2
  83.3 0.7 copy-start.4
